TPU v7x, 32 devices: a whole 2x2x4 slice. The times are simulated.
32 devices in a mesh: gx: 4 (over x, core), gy: 4 (over z), gz: 2 (over y).
Axes of the slice: x: 2, y: 2, z: 4, core: 2. Of those that a mesh axis runs over, the one named last changes fastest.
Arguments:
- divergence: float32 [64, 64, 256], P('gx', 'gy', 'gz'), may hold values from -6 to 6
- damping: float32 [64, 64, 256], P('gx', 'gy', 'gz'), may hold values from 5e-06 to 0.004
Outputs:
- potential: float32 [64, 64, 256], P('gx', 'gy', 'gz')
All inputs are finite; a program needn't handle non-finite values.
Results may differ from a plain program's by a relative error of at most 0.0001.
Values sent between devices are 32-bit elements; how exact they have to be, the bound alone decides.
A program may use at most 64 MiB of HBM per device.

v0:
```python
import math

import jax
import jax.numpy as jnp
from jax import lax
from jax.sharding import PartitionSpec as P

LEVELS = 4
POST = 2


relax_weight = 2.0 / 3.0


def with_halo(block, sides, width):
    for axis, dim in sides:
        count = lax.axis_size(axis)
        forward = [(i, i + 1) for i in range(count - 1)]
        backward = [(target, source) for source, target in forward]
        low = lax.ppermute(
            lax.slice_in_dim(block, block.shape[dim] - width, None, axis=dim), axis, forward
        )
        high = lax.ppermute(lax.slice_in_dim(block, 0, width, axis=dim), axis, backward)
        block = jnp.concatenate([low, block, high], axis=dim)
    return block


def neighbour_sum(padded):
    total = padded[2:, 1:-1, 1:-1] + padded[:-2, 1:-1, 1:-1]
    total = total + padded[1:-1, 2:, 1:-1] + padded[1:-1, :-2, 1:-1]
    total = total + padded[1:-1, 1:-1, 2:] + padded[1:-1, 1:-1, :-2]
    return total


def apply_level(values, padded, damping_level, coupling):
    return (6.0 * values - neighbour_sum(padded)) * coupling + damping_level * values


def relaxed_sweep(values, padded, source, damping_level, coupling):
    diagonal = 6.0 * coupling + damping_level
    return (
        values
        + relax_weight * (source - apply_level(values, padded, damping_level, coupling)) / diagonal
    )


def coarsen(values, block_x, block_y, block_z):
    size_x, size_y, size_z = values.shape
    shaped = values.reshape(
        size_x // block_x, block_x, size_y // block_y, block_y, size_z // block_z, block_z
    )
    return shaped.mean(axis=(1, 3, 5))


def refine(values, block_x, block_y, block_z):
    return jnp.repeat(jnp.repeat(jnp.repeat(values, block_x, 0), block_y, 1), block_z, 2)


def sine_table(points, dtype):
    indices = jnp.arange(points, dtype=dtype) + 1.0
    return math.sqrt(2.0 / (points + 1)) * jnp.sin(
        math.pi * indices[:, None] * indices[None, :] / (points + 1)
    )


def eigen_values(points, spacing, dtype):
    indices = jnp.arange(points, dtype=dtype) + 1.0
    return (2.0 - 2.0 * jnp.cos(math.pi * indices / (points + 1))) / (spacing * spacing)


def coarse_solve(source, damping_mean, spacing_x, spacing_y, spacing_z):
    size_x, size_y, size_z = source.shape
    dtype = source.dtype
    table_x = sine_table(size_x, dtype)
    table_y = sine_table(size_y, dtype)
    table_z = sine_table(size_z, dtype)
    spectrum = jnp.einsum(
        "ai,bj,ck,ijk->abc", table_x, table_y, table_z, source, precision=lax.Precision.HIGHEST
    )
    denominator = (
        eigen_values(size_x, spacing_x, dtype)[:, None, None]
        + eigen_values(size_y, spacing_y, dtype)[None, :, None]
        + eigen_values(size_z, spacing_z, dtype)[None, None, :]
        + damping_mean
    )
    spectrum = spectrum / denominator
    return jnp.einsum(
        "ia,jb,kc,abc->ijk", table_x, table_y, table_z, spectrum, precision=lax.Precision.HIGHEST
    )


def face_halo(values):
    return with_halo(values, (("gx", 0), ("gy", 1), ("gz", 2)), 1)


def trimmed(block_data, margin):
    return block_data[
        margin : block_data.shape[0] - margin,
        margin : block_data.shape[1] - margin,
        margin : block_data.shape[2] - margin,
    ]


def inside_mask(block_shape, margin, dtype):
    along_x = (
        lax.axis_index("gx") * block_shape[0]
        + jnp.arange(block_shape[0] + 2 * margin, dtype=jnp.int32)
        - margin
    )
    along_y = (
        lax.axis_index("gy") * block_shape[1]
        + jnp.arange(block_shape[1] + 2 * margin, dtype=jnp.int32)
        - margin
    )
    along_z = (
        lax.axis_index("gz") * block_shape[2]
        + jnp.arange(block_shape[2] + 2 * margin, dtype=jnp.int32)
        - margin
    )
    inside_x = (along_x >= 0) & (along_x < block_shape[0] * lax.axis_size("gx"))
    inside_y = (along_y >= 0) & (along_y < block_shape[1] * lax.axis_size("gy"))
    inside_z = (along_z >= 0) & (along_z < block_shape[2] * lax.axis_size("gz"))
    joined = inside_x[:, None, None] & inside_y[None, :, None] & inside_z[None, None, :]
    return joined.astype(dtype)


def deep_postsmooth(values, source, damping_level, coupling):
    stacked = with_halo(
        jnp.stack([values, source, damping_level]), (("gx", 1), ("gy", 2), ("gz", 3)), POST
    )
    current = stacked[0]
    source_ext = stacked[1]
    damping_ext = stacked[2]
    inside = inside_mask(values.shape, POST, values.dtype)
    for sweep_index in range(POST):
        margin = sweep_index + 1
        current = relaxed_sweep(
            trimmed(current, 1),
            current,
            trimmed(source_ext, margin),
            trimmed(damping_ext, margin),
            coupling,
        ) * trimmed(inside, margin)
    return current


def local(divergence, damping):
    cells_x, cells_y, cells_z = divergence.shape
    dampings = [damping]
    for level_index in range(1, LEVELS):
        dampings.append(coarsen(dampings[-1], 2, 2, 2))
    sources = []
    smoothed = []
    source = divergence
    for level_index in range(LEVELS):
        coupling = 0.25**level_index
        values = relax_weight * source / (6.0 * coupling + dampings[level_index])
        values = relaxed_sweep(values, face_halo(values), source, dampings[level_index], coupling)
        remainder = source - apply_level(values, face_halo(values), dampings[level_index], coupling)
        sources.append(source)
        smoothed.append(values)
        if level_index + 1 < LEVELS:
            source = coarsen(remainder, 2, 2, 2)
    payload = jnp.stack([jnp.mean(remainder), jnp.mean(dampings[-1])]).reshape(1, 2)
    coarse_table = lax.all_gather(payload, ("gx", "gy", "gz"), axis=0, tiled=True)
    count_x = lax.axis_size("gx")
    count_y = lax.axis_size("gy")
    count_z = lax.axis_size("gz")
    coarse_table = coarse_table.reshape(count_x, count_y, count_z, 2)
    solution = coarse_solve(
        coarse_table[:, :, :, 0], jnp.mean(coarse_table[:, :, :, 1]), cells_x, cells_y, cells_z
    )
    own_index = (lax.axis_index("gx") * count_y + lax.axis_index("gy")) * count_z + lax.axis_index(
        "gz"
    )
    correction = lax.dynamic_slice_in_dim(solution.reshape(-1), own_index, 1).reshape(1, 1, 1)
    for level_index in reversed(range(LEVELS)):
        coupling = 0.25**level_index
        values = smoothed[level_index] + correction
        values = deep_postsmooth(values, sources[level_index], dampings[level_index], coupling)
        if level_index > 0:
            correction = refine(values, 2, 2, 2)
    return values


def solution(mesh):
    in_specs = (P("gx", "gy", "gz"), P("gx", "gy", "gz"))
    out_specs = P("gx", "gy", "gz")
    return jax.shard_map(local, mesh=mesh, in_specs=in_specs, out_specs=out_specs, check_vma=False)
```

profile of v0, /device:TPU:0, one launch (start us, length us, event | category | flops | bytes accessed | tf_op | source)
XLA Modules:
  0.0 363.5 jit_solution(4047734892677745043)
XLA Ops:
  7.5 5.6 %collective-permute-start.3 = (f32[18,1,128]{2,1,0:T(1,128)S(1)}, f32[18,1,128]{2,1,0:T(1,128)S(1)}, u32[]{:S(2)}, u32[]{:S(2)}) collective-permute-start(f32[18,1,128]{2,1,0:T(1,128)S(1)} %get-tuple-element.27), channel_id=1, source_target_pairs={{0,2},{2,4},{4,6},{1,3},{3,5},{5,7},{8,10},{10,12},{12,14},{9,11},... | collective-permute-start | bytes 27656 | tf_op jit(solution)/shard_map/ppermute | solution.py:20
  15.9 4.6 %collective-permute-start.5 = (f32[18,18,1]{2,1,0:T(8,128)S(1)}, f32[18,18,1]{2,1,0:T(8,128)S(1)}, u32[]{:S(2)}, u32[]{:S(2)}) collective-permute-start(f32[18,18,1]{2,1,0:T(8,128)S(1)} %get-tuple-element.22), channel_id=1, source_target_pairs={{0,1},{2,3},{4,5},{6,7},{8,9},{10,11},{12,13},{14,15},{16,17},{18,... | collective-permute-start | bytes 3896 | tf_op jit(solution)/shard_map/ppermute | solution.py:20
  32.1 4.6 %collective-permute-start.9 = (f32[18,1,128]{2,1,0:T(1,128)S(1)}, f32[18,1,128]{2,1,0:T(1,128)S(1)}, u32[]{:S(2)}, u32[]{:S(2)}) collective-permute-start(f32[18,1,128]{2,1,0:T(1,128)S(1)} %get-tuple-element.25), channel_id=1, source_target_pairs={{0,2},{2,4},{4,6},{1,3},{3,5},{5,7},{8,10},{10,12},{12,14},{9,11},... | collective-permute-start | bytes 27656 | tf_op jit(solution)/shard_map/ppermute | solution.py:20
  39.5 4.6 %collective-permute-start.11 = (f32[18,18,1]{2,1,0:T(8,128)S(1)}, f32[18,18,1]{2,1,0:T(8,128)S(1)}, u32[]{:S(2)}, u32[]{:S(2)}) collective-permute-start(f32[18,18,1]{2,1,0:T(8,128)S(1)} %get-tuple-element.20), channel_id=1, source_target_pairs={{0,1},{2,3},{4,5},{6,7},{8,9},{10,11},{12,13},{14,15},{16,17},{18,... | collective-permute-start | bytes 3896 | tf_op jit(solution)/shard_map/ppermute | solution.py:20
  44.1 9.8 %reshape.416 = f32[8,2,8,2,64,2]{5,4,3,2,1,0:T(8,128)} reshape(f32[16,16,128]{2,1,0:T(8,128)S(1)} %copy-done) | data formatting | bytes 262144 | tf_op jit(solution)/shard_map/reshape | solution.py:49
  58.2 9.8 %reshape.415 = f32[8,2,8,2,64,2]{5,4,3,2,1,0:T(8,128)} reshape(f32[16,16,128]{2,1,0:T(8,128)S(1)} %fusion.15) | data formatting | bytes 262144 | tf_op jit(solution)/shard_map/reshape | solution.py:49
  78.7 4.6 %collective-permute-start.15 = (f32[10,1,64]{2,1,0:T(1,128)S(1)}, f32[10,1,64]{2,1,0:T(1,128)S(1)}, u32[]{:S(2)}, u32[]{:S(2)}) collective-permute-start(f32[10,1,64]{2,1,0:T(1,128)S(1)} %get-tuple-element.53), channel_id=1, source_target_pairs={{0,2},{2,4},{4,6},{1,3},{3,5},{5,7},{8,10},{10,12},{12,14},{9,11},... | collective-permute-start | bytes 7688 | tf_op jit(solution)/shard_map/ppermute | solution.py:20
  86.1 4.6 %collective-permute-start.17 = (f32[10,10,1]{2,1,0:T(8,128)S(1)}, f32[10,10,1]{2,1,0:T(8,128)S(1)}, u32[]{:S(2)}, u32[]{:S(2)}) collective-permute-start(f32[10,10,1]{2,1,0:T(8,128)S(1)} %get-tuple-element.43), channel_id=1, source_target_pairs={{0,1},{2,3},{4,5},{6,7},{8,9},{10,11},{12,13},{14,15},{16,17},{18,... | collective-permute-start | bytes 1208 | tf_op jit(solution)/shard_map/ppermute | solution.py:20
  94.1 4.3 %collective-permute-start.19 = (f32[1,8,64]{2,1,0:T(8,128)S(1)}, f32[1,8,64]{2,1,0:T(8,128)S(1)}, u32[]{:S(2)}, u32[]{:S(2)}) collective-permute-start(f32[1,8,64]{2,1,0:T(8,128)S(1)} %get-tuple-element.55), channel_id=1, source_target_pairs={{0,8},{8,16},{16,24},{1,9},{9,17},{17,25},{2,10},{10,18},{18,26},{... | collective-permute-start | bytes 6152 | tf_op jit(solution)/shard_map/ppermute | solution.py:20
  100.5 4.5 %collective-permute-start.21 = (f32[10,1,64]{2,1,0:T(1,128)S(1)}, f32[10,1,64]{2,1,0:T(1,128)S(1)}, u32[]{:S(2)}, u32[]{:S(2)}) collective-permute-start(f32[10,1,64]{2,1,0:T(1,128)S(1)} %get-tuple-element.51), channel_id=1, source_target_pairs={{0,2},{2,4},{4,6},{1,3},{3,5},{5,7},{8,10},{10,12},{12,14},{9,11},... | collective-permute-start | bytes 7688 | tf_op jit(solution)/shard_map/ppermute | solution.py:20
  107.8 4.6 %collective-permute-start.23 = (f32[10,10,1]{2,1,0:T(8,128)S(1)}, f32[10,10,1]{2,1,0:T(8,128)S(1)}, u32[]{:S(2)}, u32[]{:S(2)}) collective-permute-start(f32[10,10,1]{2,1,0:T(8,128)S(1)} %get-tuple-element.41), channel_id=1, source_target_pairs={{0,1},{2,3},{4,5},{6,7},{8,9},{10,11},{12,13},{14,15},{16,17},{18,... | collective-permute-start | bytes 1208 | tf_op jit(solution)/shard_map/ppermute | solution.py:20
  117.1 5.0 %collective-permute-start.25 = (f32[1,4,32]{2,1,0:T(4,128)S(1)}, f32[1,4,32]{2,1,0:T(4,128)S(1)}, u32[]{:S(2)}, u32[]{:S(2)}) collective-permute-start(f32[1,4,32]{2,1,0:T(4,128)S(1)} %get-tuple-element.85), channel_id=1, source_target_pairs={{0,8},{8,16},{16,24},{1,9},{9,17},{17,25},{2,10},{10,18},{18,26},{... | collective-permute-start | bytes 1544 | tf_op jit(solution)/shard_map/ppermute | solution.py:20
  124.2 4.5 %collective-permute-start.27 = (f32[6,1,32]{2,1,0:T(1,128)S(1)}, f32[6,1,32]{2,1,0:T(1,128)S(1)}, u32[]{:S(2)}, u32[]{:S(2)}) collective-permute-start(f32[6,1,32]{2,1,0:T(1,128)S(1)} %get-tuple-element.73), channel_id=1, source_target_pairs={{0,2},{2,4},{4,6},{1,3},{3,5},{5,7},{8,10},{10,12},{12,14},{9,11},... | collective-permute-start | bytes 2312 | tf_op jit(solution)/shard_map/ppermute | solution.py:20
  131.5 4.5 %collective-permute-start.29 = (f32[6,6,1]{2,1,0:T(8,128)S(1)}, f32[6,6,1]{2,1,0:T(8,128)S(1)}, u32[]{:S(2)}, u32[]{:S(2)}) collective-permute-start(f32[6,6,1]{2,1,0:T(8,128)S(1)} %get-tuple-element.68), channel_id=1, source_target_pairs={{0,1},{2,3},{4,5},{6,7},{8,9},{10,11},{12,13},{14,15},{16,17},{18,... | collective-permute-start | bytes 440 | tf_op jit(solution)/shard_map/ppermute | solution.py:20
  139.0 5.0 %collective-permute-start.31 = (f32[1,4,32]{2,1,0:T(4,128)S(1)}, f32[1,4,32]{2,1,0:T(4,128)S(1)}, u32[]{:S(2)}, u32[]{:S(2)}) collective-permute-start(f32[1,4,32]{2,1,0:T(4,128)S(1)} %get-tuple-element.79), channel_id=1, source_target_pairs={{0,8},{8,16},{16,24},{1,9},{9,17},{17,25},{2,10},{10,18},{18,26},{... | collective-permute-start | bytes 1544 | tf_op jit(solution)/shard_map/ppermute | solution.py:20
  146.1 4.5 %collective-permute-start.33 = (f32[6,1,32]{2,1,0:T(1,128)S(1)}, f32[6,1,32]{2,1,0:T(1,128)S(1)}, u32[]{:S(2)}, u32[]{:S(2)}) collective-permute-start(f32[6,1,32]{2,1,0:T(1,128)S(1)} %get-tuple-element.71), channel_id=1, source_target_pairs={{0,2},{2,4},{4,6},{1,3},{3,5},{5,7},{8,10},{10,12},{12,14},{9,11},... | collective-permute-start | bytes 2312 | tf_op jit(solution)/shard_map/ppermute | solution.py:20
  153.3 4.5 %collective-permute-start.35 = (f32[6,6,1]{2,1,0:T(8,128)S(1)}, f32[6,6,1]{2,1,0:T(8,128)S(1)}, u32[]{:S(2)}, u32[]{:S(2)}) collective-permute-start(f32[6,6,1]{2,1,0:T(8,128)S(1)} %get-tuple-element.66), channel_id=1, source_target_pairs={{0,1},{2,3},{4,5},{6,7},{8,9},{10,11},{12,13},{14,15},{16,17},{18,... | collective-permute-start | bytes 440 | tf_op jit(solution)/shard_map/ppermute | solution.py:20
  161.6 5.0 %collective-permute-start.37 = (f32[1,2,16]{2,1,0:T(2,128)S(1)}, f32[1,2,16]{2,1,0:T(2,128)S(1)}, u32[]{:S(2)}, u32[]{:S(2)}) collective-permute-start(f32[1,2,16]{2,1,0:T(2,128)S(1)} %get-tuple-element.97), channel_id=1, source_target_pairs={{0,8},{8,16},{16,24},{1,9},{9,17},{17,25},{2,10},{10,18},{18,26},{... | collective-permute-start | bytes 392 | tf_op jit(solution)/shard_map/ppermute | solution.py:20
  168.7 4.5 %collective-permute-start.39 = (f32[4,1,16]{2,1,0:T(1,128)S(1)}, f32[4,1,16]{2,1,0:T(1,128)S(1)}, u32[]{:S(2)}, u32[]{:S(2)}) collective-permute-start(f32[4,1,16]{2,1,0:T(1,128)S(1)} %get-tuple-element.89), channel_id=1, source_target_pairs={{0,2},{2,4},{4,6},{1,3},{3,5},{5,7},{8,10},{10,12},{12,14},{9,11},... | collective-permute-start | bytes 776 | tf_op jit(solution)/shard_map/ppermute | solution.py:20
  175.9 4.5 %collective-permute-start.41 = (f32[4,4,1]{2,1,0:T(4,128)S(1)}, f32[4,4,1]{2,1,0:T(4,128)S(1)}, u32[]{:S(2)}, u32[]{:S(2)}) collective-permute-start(f32[4,4,1]{2,1,0:T(4,128)S(1)} %get-tuple-element.78), channel_id=1, source_target_pairs={{0,1},{2,3},{4,5},{6,7},{8,9},{10,11},{12,13},{14,15},{16,17},{18,... | collective-permute-start | bytes 200 | tf_op jit(solution)/shard_map/ppermute | solution.py:20
  183.2 5.0 %collective-permute-start.43 = (f32[1,2,16]{2,1,0:T(2,128)S(1)}, f32[1,2,16]{2,1,0:T(2,128)S(1)}, u32[]{:S(2)}, u32[]{:S(2)}) collective-permute-start(f32[1,2,16]{2,1,0:T(2,128)S(1)} %get-tuple-element.91), channel_id=1, source_target_pairs={{0,8},{8,16},{16,24},{1,9},{9,17},{17,25},{2,10},{10,18},{18,26},{... | collective-permute-start | bytes 392 | tf_op jit(solution)/shard_map/ppermute | solution.py:20
  190.3 4.5 %collective-permute-start.45 = (f32[4,1,16]{2,1,0:T(1,128)S(1)}, f32[4,1,16]{2,1,0:T(1,128)S(1)}, u32[]{:S(2)}, u32[]{:S(2)}) collective-permute-start(f32[4,1,16]{2,1,0:T(1,128)S(1)} %get-tuple-element.87), channel_id=1, source_target_pairs={{0,2},{2,4},{4,6},{1,3},{3,5},{5,7},{8,10},{10,12},{12,14},{9,11},... | collective-permute-start | bytes 776 | tf_op jit(solution)/shard_map/ppermute | solution.py:20
  197.5 4.5 %collective-permute-start.47 = (f32[4,4,1]{2,1,0:T(4,128)S(1)}, f32[4,4,1]{2,1,0:T(4,128)S(1)}, u32[]{:S(2)}, u32[]{:S(2)}) collective-permute-start(f32[4,4,1]{2,1,0:T(4,128)S(1)} %get-tuple-element.76), channel_id=1, source_target_pairs={{0,1},{2,3},{4,5},{6,7},{8,9},{10,11},{12,13},{14,15},{16,17},{18,... | collective-permute-start | bytes 200 | tf_op jit(solution)/shard_map/ppermute | solution.py:20
  205.0 47.4 %all-reduce = f32[64]{0:T(128)S(1)} all-reduce(f32[64]{0:T(128)S(1)} %maximum_dynamic-update-slice_fusion), channel_id=2, replica_groups=mesh['gx'=4,'gy'=4,'gz'=2] {'gx','gy','gz'}, use_global_device_ids=true, to_apply=%add | all-reduce | flops 64 | bytes 512
  269.2 4.2 %collective-permute-done.51 = f32[3,6,2,16]{3,2,1,0:T(2,128)S(1)} collective-permute-done((f32[3,6,2,16]{3,2,1,0:T(2,128)S(1)}, f32[3,6,2,16]{3,2,1,0:T(2,128)S(1)}, u32[]{:S(2)}, u32[]{:S(2)}) %collective-permute-start.51) | collective-permute-done | bytes 2336 | tf_op jit(solution)/shard_map/ppermute | solution.py:23
  278.3 4.1 %collective-permute-done.53 = f32[3,6,6,2]{3,2,1,0:T(8,128)S(1)} collective-permute-done((f32[3,6,6,2]{3,2,1,0:T(8,128)S(1)}, f32[3,6,6,2]{3,2,1,0:T(8,128)S(1)}, u32[]{:S(2)}, u32[]{:S(2)}) %collective-permute-start.53) | collective-permute-done | bytes 896 | tf_op jit(solution)/shard_map/ppermute | solution.py:23
  294.2 4.2 %collective-permute-done.57 = f32[3,8,2,32]{3,2,1,0:T(2,128)S(1)} collective-permute-done((f32[3,8,2,32]{3,2,1,0:T(2,128)S(1)}, f32[3,8,2,32]{3,2,1,0:T(2,128)S(1)}, u32[]{:S(2)}, u32[]{:S(2)}) %collective-permute-start.57) | collective-permute-done | bytes 6176 | tf_op jit(solution)/shard_map/ppermute | solution.py:23
  303.2 4.2 %collective-permute-done.59 = f32[3,8,8,2]{3,2,1,0:T(8,128)S(1)} collective-permute-done((f32[3,8,8,2]{3,2,1,0:T(8,128)S(1)}, f32[3,8,8,2]{3,2,1,0:T(8,128)S(1)}, u32[]{:S(2)}, u32[]{:S(2)}) %collective-permute-start.59) | collective-permute-done | bytes 1568 | tf_op jit(solution)/shard_map/ppermute | solution.py:23
  318.0 4.2 %collective-permute-done.63 = f32[3,12,2,64]{3,2,1,0:T(2,128)S(1)} collective-permute-done((f32[3,12,2,64]{3,2,1,0:T(2,128)S(1)}, f32[3,12,2,64]{3,2,1,0:T(2,128)S(1)}, u32[]{:S(2)}, u32[]{:S(2)}) %collective-permute-start.63) | collective-permute-done | bytes 18464 | tf_op jit(solution)/shard_map/ppermute | solution.py:23
  325.3 5.8 %collective-permute-done.64 = f32[3,12,12,2]{3,2,1,0:T(8,128)S(1)} collective-permute-done((f32[3,12,12,2]{3,2,1,0:T(8,128)S(1)}, f32[3,12,12,2]{3,2,1,0:T(8,128)S(1)}, u32[]{:S(2)}, u32[]{:S(2)}) %collective-permute-start.64) | collective-permute-done | bytes 3488 | tf_op jit(solution)/shard_map/ppermute | solution.py:20
  331.2 4.5 %collective-permute-done.65 = f32[3,12,12,2]{3,2,1,0:T(8,128)S(1)} collective-permute-done((f32[3,12,12,2]{3,2,1,0:T(8,128)S(1)}, f32[3,12,12,2]{3,2,1,0:T(8,128)S(1)}, u32[]{:S(2)}, u32[]{:S(2)}) %collective-permute-start.65) | collective-permute-done | bytes 3488 | tf_op jit(solution)/shard_map/ppermute | solution.py:23
  346.2 4.3 %collective-permute-done.69 = f32[3,20,2,128]{3,2,1,0:T(2,128)S(1)} collective-permute-done((f32[3,20,2,128]{3,2,1,0:T(2,128)S(1)}, f32[3,20,2,128]{3,2,1,0:T(2,128)S(1)}, u32[]{:S(2)}, u32[]{:S(2)}) %collective-permute-start.69) | collective-permute-done | bytes 61472 | tf_op jit(solution)/shard_map/ppermute | solution.py:23
  (269 shorter events, 159.4 us)
Async XLA Ops:
  6.2 6.9 %collective-permute-start.2 = (f32[18,1,128]{2,1,0:T(1,128)S(1)}, f32[18,1,128]{2,1,0:T(1,128)S(1)}, u32[]{:S(2)}, u32[]{:S(2)}) collective-permute-start(f32[18,1,128]{2,1,0:T(1,128)S(1)} %get-tuple-element.28), channel_id=1, source_target_pairs={{2,0},{4,2},{6,4},{3,1},{5,3},{7,5},{10,8},{12,10},{14,12},{11,9},... | collective-permute-start | bytes 27656 | tf_op jit(solution)/shard_map/ppermute | solution.py:23
  7.5 7.0 %collective-permute-start.3 = (f32[18,1,128]{2,1,0:T(1,128)S(1)}, f32[18,1,128]{2,1,0:T(1,128)S(1)}, u32[]{:S(2)}, u32[]{:S(2)}) collective-permute-start(f32[18,1,128]{2,1,0:T(1,128)S(1)} %get-tuple-element.27), channel_id=1, source_target_pairs={{0,2},{2,4},{4,6},{1,3},{3,5},{5,7},{8,10},{10,12},{12,14},{9,11},... | collective-permute-start | bytes 27656 | tf_op jit(solution)/shard_map/ppermute | solution.py:20
  14.6 9.6 %collective-permute-start.4 = (f32[18,18,1]{2,1,0:T(8,128)S(1)}, f32[18,18,1]{2,1,0:T(8,128)S(1)}, u32[]{:S(2)}, u32[]{:S(2)}) collective-permute-start(f32[18,18,1]{2,1,0:T(8,128)S(1)} %get-tuple-element.21), channel_id=1, source_target_pairs={{1,0},{3,2},{5,4},{7,6},{9,8},{11,10},{13,12},{15,14},{17,16},{19,... | collective-permute-start | bytes 3896 | tf_op jit(solution)/shard_map/ppermute | solution.py:23
  15.9 9.5 %collective-permute-start.5 = (f32[18,18,1]{2,1,0:T(8,128)S(1)}, f32[18,18,1]{2,1,0:T(8,128)S(1)}, u32[]{:S(2)}, u32[]{:S(2)}) collective-permute-start(f32[18,18,1]{2,1,0:T(8,128)S(1)} %get-tuple-element.22), channel_id=1, source_target_pairs={{0,1},{2,3},{4,5},{6,7},{8,9},{10,11},{12,13},{14,15},{16,17},{18,... | collective-permute-start | bytes 3896 | tf_op jit(solution)/shard_map/ppermute | solution.py:20
  32.1 5.9 %collective-permute-start.9 = (f32[18,1,128]{2,1,0:T(1,128)S(1)}, f32[18,1,128]{2,1,0:T(1,128)S(1)}, u32[]{:S(2)}, u32[]{:S(2)}) collective-permute-start(f32[18,1,128]{2,1,0:T(1,128)S(1)} %get-tuple-element.25), channel_id=1, source_target_pairs={{0,2},{2,4},{4,6},{1,3},{3,5},{5,7},{8,10},{10,12},{12,14},{9,11},... | collective-permute-start | bytes 27656 | tf_op jit(solution)/shard_map/ppermute | solution.py:20
  38.2 19.7 %collective-permute-start.10 = (f32[18,18,1]{2,1,0:T(8,128)S(1)}, f32[18,18,1]{2,1,0:T(8,128)S(1)}, u32[]{:S(2)}, u32[]{:S(2)}) collective-permute-start(f32[18,18,1]{2,1,0:T(8,128)S(1)} %get-tuple-element.19), channel_id=1, source_target_pairs={{1,0},{3,2},{5,4},{7,6},{9,8},{11,10},{13,12},{15,14},{17,16},{19,... | collective-permute-start | bytes 3896 | tf_op jit(solution)/shard_map/ppermute | solution.py:23
  39.5 18.4 %collective-permute-start.11 = (f32[18,18,1]{2,1,0:T(8,128)S(1)}, f32[18,18,1]{2,1,0:T(8,128)S(1)}, u32[]{:S(2)}, u32[]{:S(2)}) collective-permute-start(f32[18,18,1]{2,1,0:T(8,128)S(1)} %get-tuple-element.20), channel_id=1, source_target_pairs={{0,1},{2,3},{4,5},{6,7},{8,9},{10,11},{12,13},{14,15},{16,17},{18,... | collective-permute-start | bytes 3896 | tf_op jit(solution)/shard_map/ppermute | solution.py:20
  77.4 5.9 %collective-permute-start.14 = (f32[10,1,64]{2,1,0:T(1,128)S(1)}, f32[10,1,64]{2,1,0:T(1,128)S(1)}, u32[]{:S(2)}, u32[]{:S(2)}) collective-permute-start(f32[10,1,64]{2,1,0:T(1,128)S(1)} %get-tuple-element.54), channel_id=1, source_target_pairs={{2,0},{4,2},{6,4},{3,1},{5,3},{7,5},{10,8},{12,10},{14,12},{11,9},... | collective-permute-start | bytes 7688 | tf_op jit(solution)/shard_map/ppermute | solution.py:23
  78.7 5.9 %collective-permute-start.15 = (f32[10,1,64]{2,1,0:T(1,128)S(1)}, f32[10,1,64]{2,1,0:T(1,128)S(1)}, u32[]{:S(2)}, u32[]{:S(2)}) collective-permute-start(f32[10,1,64]{2,1,0:T(1,128)S(1)} %get-tuple-element.53), channel_id=1, source_target_pairs={{0,2},{2,4},{4,6},{1,3},{3,5},{5,7},{8,10},{10,12},{12,14},{9,11},... | collective-permute-start | bytes 7688 | tf_op jit(solution)/shard_map/ppermute | solution.py:20
  84.8 6.3 %collective-permute-start.16 = (f32[10,10,1]{2,1,0:T(8,128)S(1)}, f32[10,10,1]{2,1,0:T(8,128)S(1)}, u32[]{:S(2)}, u32[]{:S(2)}) collective-permute-start(f32[10,10,1]{2,1,0:T(8,128)S(1)} %get-tuple-element.42), channel_id=1, source_target_pairs={{1,0},{3,2},{5,4},{7,6},{9,8},{11,10},{13,12},{15,14},{17,16},{19,... | collective-permute-start | bytes 1208 | tf_op jit(solution)/shard_map/ppermute | solution.py:23
  86.1 6.6 %collective-permute-start.17 = (f32[10,10,1]{2,1,0:T(8,128)S(1)}, f32[10,10,1]{2,1,0:T(8,128)S(1)}, u32[]{:S(2)}, u32[]{:S(2)}) collective-permute-start(f32[10,10,1]{2,1,0:T(8,128)S(1)} %get-tuple-element.43), channel_id=1, source_target_pairs={{0,1},{2,3},{4,5},{6,7},{8,9},{10,11},{12,13},{14,15},{16,17},{18,... | collective-permute-start | bytes 1208 | tf_op jit(solution)/shard_map/ppermute | solution.py:20
  99.2 5.9 %collective-permute-start.20 = (f32[10,1,64]{2,1,0:T(1,128)S(1)}, f32[10,1,64]{2,1,0:T(1,128)S(1)}, u32[]{:S(2)}, u32[]{:S(2)}) collective-permute-start(f32[10,1,64]{2,1,0:T(1,128)S(1)} %get-tuple-element.52), channel_id=1, source_target_pairs={{2,0},{4,2},{6,4},{3,1},{5,3},{7,5},{10,8},{12,10},{14,12},{11,9},... | collective-permute-start | bytes 7688 | tf_op jit(solution)/shard_map/ppermute | solution.py:23
  106.5 7.2 %collective-permute-start.22 = (f32[10,10,1]{2,1,0:T(8,128)S(1)}, f32[10,10,1]{2,1,0:T(8,128)S(1)}, u32[]{:S(2)}, u32[]{:S(2)}) collective-permute-start(f32[10,10,1]{2,1,0:T(8,128)S(1)} %get-tuple-element.40), channel_id=1, source_target_pairs={{1,0},{3,2},{5,4},{7,6},{9,8},{11,10},{13,12},{15,14},{17,16},{19,... | collective-permute-start | bytes 1208 | tf_op jit(solution)/shard_map/ppermute | solution.py:23
  107.8 6.6 %collective-permute-start.23 = (f32[10,10,1]{2,1,0:T(8,128)S(1)}, f32[10,10,1]{2,1,0:T(8,128)S(1)}, u32[]{:S(2)}, u32[]{:S(2)}) collective-permute-start(f32[10,10,1]{2,1,0:T(8,128)S(1)} %get-tuple-element.41), channel_id=1, source_target_pairs={{0,1},{2,3},{4,5},{6,7},{8,9},{10,11},{12,13},{14,15},{16,17},{18,... | collective-permute-start | bytes 1208 | tf_op jit(solution)/shard_map/ppermute | solution.py:20
  115.8 6.4 %collective-permute-start.24 = (f32[1,4,32]{2,1,0:T(4,128)S(1)}, f32[1,4,32]{2,1,0:T(4,128)S(1)}, u32[]{:S(2)}, u32[]{:S(2)}) collective-permute-start(f32[1,4,32]{2,1,0:T(4,128)S(1)} %get-tuple-element.86), channel_id=1, source_target_pairs={{8,0},{16,8},{24,16},{9,1},{17,9},{25,17},{10,2},{18,10},{26,18},{... | collective-permute-start | bytes 1544 | tf_op jit(solution)/shard_map/ppermute | solution.py:23
  122.9 5.9 %collective-permute-start.26 = (f32[6,1,32]{2,1,0:T(1,128)S(1)}, f32[6,1,32]{2,1,0:T(1,128)S(1)}, u32[]{:S(2)}, u32[]{:S(2)}) collective-permute-start(f32[6,1,32]{2,1,0:T(1,128)S(1)} %get-tuple-element.74), channel_id=1, source_target_pairs={{2,0},{4,2},{6,4},{3,1},{5,3},{7,5},{10,8},{12,10},{14,12},{11,9},... | collective-permute-start | bytes 2312 | tf_op jit(solution)/shard_map/ppermute | solution.py:23
  131.5 6.1 %collective-permute-start.29 = (f32[6,6,1]{2,1,0:T(8,128)S(1)}, f32[6,6,1]{2,1,0:T(8,128)S(1)}, u32[]{:S(2)}, u32[]{:S(2)}) collective-permute-start(f32[6,6,1]{2,1,0:T(8,128)S(1)} %get-tuple-element.68), channel_id=1, source_target_pairs={{0,1},{2,3},{4,5},{6,7},{8,9},{10,11},{12,13},{14,15},{16,17},{18,... | collective-permute-start | bytes 440 | tf_op jit(solution)/shard_map/ppermute | solution.py:20
  137.7 6.4 %collective-permute-start.30 = (f32[1,4,32]{2,1,0:T(4,128)S(1)}, f32[1,4,32]{2,1,0:T(4,128)S(1)}, u32[]{:S(2)}, u32[]{:S(2)}) collective-permute-start(f32[1,4,32]{2,1,0:T(4,128)S(1)} %get-tuple-element.80), channel_id=1, source_target_pairs={{8,0},{16,8},{24,16},{9,1},{17,9},{25,17},{10,2},{18,10},{26,18},{... | collective-permute-start | bytes 1544 | tf_op jit(solution)/shard_map/ppermute | solution.py:23
  144.8 6.0 %collective-permute-start.32 = (f32[6,1,32]{2,1,0:T(1,128)S(1)}, f32[6,1,32]{2,1,0:T(1,128)S(1)}, u32[]{:S(2)}, u32[]{:S(2)}) collective-permute-start(f32[6,1,32]{2,1,0:T(1,128)S(1)} %get-tuple-element.72), channel_id=1, source_target_pairs={{2,0},{4,2},{6,4},{3,1},{5,3},{7,5},{10,8},{12,10},{14,12},{11,9},... | collective-permute-start | bytes 2312 | tf_op jit(solution)/shard_map/ppermute | solution.py:23
  152.0 5.9 %collective-permute-start.34 = (f32[6,6,1]{2,1,0:T(8,128)S(1)}, f32[6,6,1]{2,1,0:T(8,128)S(1)}, u32[]{:S(2)}, u32[]{:S(2)}) collective-permute-start(f32[6,6,1]{2,1,0:T(8,128)S(1)} %get-tuple-element.65), channel_id=1, source_target_pairs={{1,0},{3,2},{5,4},{7,6},{9,8},{11,10},{13,12},{15,14},{17,16},{19,... | collective-permute-start | bytes 440 | tf_op jit(solution)/shard_map/ppermute | solution.py:23
  153.3 6.1 %collective-permute-start.35 = (f32[6,6,1]{2,1,0:T(8,128)S(1)}, f32[6,6,1]{2,1,0:T(8,128)S(1)}, u32[]{:S(2)}, u32[]{:S(2)}) collective-permute-start(f32[6,6,1]{2,1,0:T(8,128)S(1)} %get-tuple-element.66), channel_id=1, source_target_pairs={{0,1},{2,3},{4,5},{6,7},{8,9},{10,11},{12,13},{14,15},{16,17},{18,... | collective-permute-start | bytes 440 | tf_op jit(solution)/shard_map/ppermute | solution.py:20
  160.3 6.3 %collective-permute-start.36 = (f32[1,2,16]{2,1,0:T(2,128)S(1)}, f32[1,2,16]{2,1,0:T(2,128)S(1)}, u32[]{:S(2)}, u32[]{:S(2)}) collective-permute-start(f32[1,2,16]{2,1,0:T(2,128)S(1)} %get-tuple-element.98), channel_id=1, source_target_pairs={{8,0},{16,8},{24,16},{9,1},{17,9},{25,17},{10,2},{18,10},{26,18},{... | collective-permute-start | bytes 392 | tf_op jit(solution)/shard_map/ppermute | solution.py:23
  175.9 5.9 %collective-permute-start.41 = (f32[4,4,1]{2,1,0:T(4,128)S(1)}, f32[4,4,1]{2,1,0:T(4,128)S(1)}, u32[]{:S(2)}, u32[]{:S(2)}) collective-permute-start(f32[4,4,1]{2,1,0:T(4,128)S(1)} %get-tuple-element.78), channel_id=1, source_target_pairs={{0,1},{2,3},{4,5},{6,7},{8,9},{10,11},{12,13},{14,15},{16,17},{18,... | collective-permute-start | bytes 200 | tf_op jit(solution)/shard_map/ppermute | solution.py:20
  181.9 6.3 %collective-permute-start.42 = (f32[1,2,16]{2,1,0:T(2,128)S(1)}, f32[1,2,16]{2,1,0:T(2,128)S(1)}, u32[]{:S(2)}, u32[]{:S(2)}) collective-permute-start(f32[1,2,16]{2,1,0:T(2,128)S(1)} %get-tuple-element.92), channel_id=1, source_target_pairs={{8,0},{16,8},{24,16},{9,1},{17,9},{25,17},{10,2},{18,10},{26,18},{... | collective-permute-start | bytes 392 | tf_op jit(solution)/shard_map/ppermute | solution.py:23
  189.0 6.5 %collective-permute-start.44 = (f32[4,1,16]{2,1,0:T(1,128)S(1)}, f32[4,1,16]{2,1,0:T(1,128)S(1)}, u32[]{:S(2)}, u32[]{:S(2)}) collective-permute-start(f32[4,1,16]{2,1,0:T(1,128)S(1)} %get-tuple-element.88), channel_id=1, source_target_pairs={{2,0},{4,2},{6,4},{3,1},{5,3},{7,5},{10,8},{12,10},{14,12},{11,9},... | collective-permute-start | bytes 776 | tf_op jit(solution)/shard_map/ppermute | solution.py:23
  197.5 5.9 %collective-permute-start.47 = (f32[4,4,1]{2,1,0:T(4,128)S(1)}, f32[4,4,1]{2,1,0:T(4,128)S(1)}, u32[]{:S(2)}, u32[]{:S(2)}) collective-permute-start(f32[4,4,1]{2,1,0:T(4,128)S(1)} %get-tuple-element.76), channel_id=1, source_target_pairs={{0,1},{2,3},{4,5},{6,7},{8,9},{10,11},{12,13},{14,15},{16,17},{18,... | collective-permute-start | bytes 200 | tf_op jit(solution)/shard_map/ppermute | solution.py:20
  275.6 6.7 %collective-permute-start.53 = (f32[3,6,6,2]{3,2,1,0:T(8,128)S(1)}, f32[3,6,6,2]{3,2,1,0:T(8,128)S(1)}, u32[]{:S(2)}, u32[]{:S(2)}) collective-permute-start(f32[3,6,6,2]{3,2,1,0:T(8,128)S(1)} %get-tuple-element.48), channel_id=1, source_target_pairs={{1,0},{3,2},{5,4},{7,6},{9,8},{11,10},{13,12},{15,14},{17,16},{19,... | collective-permute-start | bytes 2600 | tf_op jit(solution)/shard_map/ppermute | solution.py:23
  300.1 7.3 %collective-permute-start.59 = (f32[3,8,8,2]{3,2,1,0:T(8,128)S(1)}, f32[3,8,8,2]{3,2,1,0:T(8,128)S(1)}, u32[]{:S(2)}, u32[]{:S(2)}) collective-permute-start(f32[3,8,8,2]{3,2,1,0:T(8,128)S(1)} %get-tuple-element.39), channel_id=1, source_target_pairs={{1,0},{3,2},{5,4},{7,6},{9,8},{11,10},{13,12},{15,14},{17,16},{19,... | collective-permute-start | bytes 4616 | tf_op jit(solution)/shard_map/ppermute | solution.py:23
  322.5 8.7 %collective-permute-start.64 = (f32[3,12,12,2]{3,2,1,0:T(8,128)S(1)}, f32[3,12,12,2]{3,2,1,0:T(8,128)S(1)}, u32[]{:S(2)}, u32[]{:S(2)}) collective-permute-start(f32[3,12,12,2]{3,2,1,0:T(8,128)S(1)} %get-tuple-element.17), channel_id=1, source_target_pairs={{0,1},{2,3},{4,5},{6,7},{8,9},{10,11},{12,13},{14,15},{16,17},{18,... | collective-permute-start | bytes 10376 | tf_op jit(solution)/shard_map/ppermute | solution.py:20
  324.0 11.7 %collective-permute-start.65 = (f32[3,12,12,2]{3,2,1,0:T(8,128)S(1)}, f32[3,12,12,2]{3,2,1,0:T(8,128)S(1)}, u32[]{:S(2)}, u32[]{:S(2)}) collective-permute-start(f32[3,12,12,2]{3,2,1,0:T(8,128)S(1)} %get-tuple-element.18), channel_id=1, source_target_pairs={{1,0},{3,2},{5,4},{7,6},{9,8},{11,10},{13,12},{15,14},{17,16},{19,... | collective-permute-start | bytes 10376 | tf_op jit(solution)/shard_map/ppermute | solution.py:23
  344.4 6.1 %collective-permute-start.69 = (f32[3,20,2,128]{3,2,1,0:T(2,128)S(1)}, f32[3,20,2,128]{3,2,1,0:T(2,128)S(1)}, u32[]{:S(2)}, u32[]{:S(2)}) collective-permute-start(f32[3,20,2,128]{3,2,1,0:T(2,128)S(1)} %get-tuple-element.11), channel_id=1, source_target_pairs={{2,0},{4,2},{6,4},{3,1},{5,3},{7,5},{10,8},{12,10},{14,12},{11,9},... | collective-permute-start | bytes 184328 | tf_op jit(solution)/shard_map/ppermute | solution.py:23
  353.5 6.4 %collective-permute-start.71 = (f32[3,20,20,2]{2,3,1,0:T(2,128)S(1)}, f32[3,20,20,2]{2,3,1,0:T(2,128)S(1)}, u32[]{:S(2)}, u32[]{:S(2)}) collective-permute-start(f32[3,20,20,2]{2,3,1,0:T(2,128)S(1)} %copy.360), channel_id=1, source_target_pairs={{1,0},{3,2},{5,4},{7,6},{9,8},{11,10},{13,12},{15,14},{17,16},{19,... | collective-permute-start | bytes 28808 | tf_op jit(solution)/shard_map/ppermute | solution.py:23
  (42 other events, 246.5 us)
where the time goes:
time: 366 us; the launch traced here: 364 us
  starting transfers between devices  179 us (49%)
  waiting for transfers between devices  85.3 us (23%)
  blocking collectives  47.4 us (13%)
  local copies, waits for them, and re-layouts  27.7 us (8%)
  other arithmetic  19.6 us (5%)
    ppermute x36, starting transfers between devices, with_halo(): lax.ppermute(lax.slice_in_dim(block, block.shape[dim] - width, None, axis...  132 us
    ppermute x36, waiting for transfers between devices, with_halo(): lax.ppermute(lax.slice_in_dim(block, 0, width, axis=dim), axis, backward)  50.3 us
    unnamed x1, blocking collectives  47.4 us
    ppermute x36, starting transfers between devices, with_halo(): lax.ppermute(lax.slice_in_dim(block, 0, width, axis=dim), axis, backward)  46.6 us
    ppermute x36, waiting for transfers between devices, with_halo(): lax.ppermute(lax.slice_in_dim(block, block.shape[dim] - width, None, axis...  35.1 us
    reshape x4, local copies, waits for them, and re-layouts, coarsen(): values.reshape(size_x // block_x, block_x, size_y // block_y, block_y, si...  20.8 us
    reduce_sum x6, other arithmetic, coarsen(): return shaped.mean(axis=(1, 3, 5))  8.56 us
  transfers between devices with their start and end apart: 72, of which 45 were waited for; matrix products, arithmetic and copies ran while one was open for 5% of the time, Pallas kernels for 0%

commit v1 on v0

v1 whole, which is shorter than its diff:
```python
import functools
import math

import jax
import jax.numpy as jnp
import numpy as np
from jax import lax
from jax.experimental import pallas as pl
from jax.experimental.pallas import tpu as pltpu
from jax.sharding import PartitionSpec as P

AXES = ("gx", "gy", "gz")
ROUNDS = 7
WEIGHT = 2.0 / 3.0
MESH = pl.DeviceIdType.MESH
HIGH = lax.Precision.HIGHEST


def dot(a, b, dims=(((1,), (0,)), ((), ()))):
    return lax.dot_general(a, b, dims, precision=HIGH, preferred_element_type=jnp.float32)


def one_hot(condition):
    return jnp.where(condition, 1.0, 0.0).astype(jnp.float32)


def iota(shape, dim):
    return lax.broadcasted_iota(jnp.int32, shape, dim)


def coarsen_dup(values, step):
    nx, ny, nz = values.shape
    pairs = values.reshape(nx // 2, 2, ny, nz)
    total = pairs[:, 0] + pairs[:, 1]
    for dim, size in ((1, ny), (2, nz)):
        even = (iota(total.shape, dim) // step) % 2 == 0
        total = total + jnp.where(
            even, pltpu.roll(total, size - step, dim), pltpu.roll(total, step, dim)
        )
    return total * 0.125


def expand_x(values, times):
    nx, ny, nz = values.shape
    return jnp.broadcast_to(values[:, None], (nx, times, ny, nz)).reshape(nx * times, ny, nz)


def sum_x(values, low, high):
    return jnp.concatenate([low[None], values[:-1]], 0) + jnp.concatenate(
        [values[1:], high[None]], 0
    )


def neighbours_global(values, step, valid_z):
    nx, ny, nz = values.shape
    zero = jnp.zeros((ny, nz), jnp.float32)
    total = sum_x(values, zero, zero)
    row, lane = iota(values.shape, 1), iota(values.shape, 2)
    total = total + jnp.where(row < step, 0.0, pltpu.roll(values, step, 1))
    total = total + jnp.where(row >= ny - step, 0.0, pltpu.roll(values, ny - step, 1))
    total = total + jnp.where(lane < step, 0.0, pltpu.roll(values, step, 2))
    total = total + jnp.where(lane >= valid_z - step, 0.0, pltpu.roll(values, nz - step, 2))
    return total


def kernel(
    counts, tables, b_ref, d_ref, ty_ref, tz_ref, den_ref, out_ref,
    xsend, ysend, zsend, xrecv, yrecv, zrecv, pay, gathered, gb, gd, v2,
    ssem, rsem, gssem, grsem,
):
    cx, cy, cz = counts
    table_x = tables
    nx, ny, nz = (lax.axis_size(a) for a in AXES)
    devices = nx * ny * nz
    gx, gy, gz = (lax.axis_index(a) for a in AXES)
    place = {"gx": gx, "gy": gy, "gz": gz}
    size = {"gx": nx, "gy": ny, "gz": nz}
    me = (gx * ny + gy) * nz + gz

    def coords(index):
        return (index // (ny * nz), (index // nz) % ny, index % nz)

    xrecv[...] = jnp.zeros_like(xrecv)
    yrecv[...] = jnp.zeros_like(yrecv)
    zrecv[...] = jnp.zeros_like(zrecv)

    barrier = pltpu.get_barrier_semaphore()

    @pl.loop(1, devices)
    def _(k):
        pl.semaphore_signal(
            barrier, inc=1, device_id=coords((me + k) % devices), device_id_type=MESH
        )

    b0 = b_ref[...]
    d0 = d_ref[...]

    pl.semaphore_wait(barrier, devices - 1)

    def copies(r, level_x):
        result = []
        for axis_number, (axis, send, recv, length) in enumerate(
            (("gx", xsend, xrecv, cy), ("gy", ysend, yrecv, level_x), ("gz", zsend, zrecv, None))
        ):
            for side in (0, 1):
                other = 1 - side
                index = 2 * axis_number
                if length is None:
                    src = send.at[r]
                    there, here = recv.at[r, other], recv.at[r, side]
                    if level_x * cy < send.shape[2]:
                        cut = (slice(None), pl.ds(0, level_x * cy))
                        src, there, here = src.at[cut], there.at[cut], here.at[cut]
                else:
                    cut = pl.ds(0, length)
                    src = send.at[r, side, cut]
                    there, here = recv.at[r, other, cut], recv.at[r, side, cut]
                target = dict(place)
                target[axis] = place[axis] + (1 if side else -1)
                device = tuple(target[a] for a in AXES)
                exists = place[axis] < size[axis] - 1 if side else place[axis] > 0
                out = pltpu.make_async_remote_copy(
                    src, there, ssem.at[r, index + side], rsem.at[r, index + other], device, MESH
                )
                back = pltpu.make_async_remote_copy(
                    src, here, ssem.at[r, index + side], rsem.at[r, index + side], device, MESH
                )
                result.append((exists, out, back))
        return result

    def exchange(r, values):
        level_x = values.shape[0]
        rows = level_x * cy
        xsend[r, 0] = values[0]
        xsend[r, 1] = values[-1]
        ysend[r, 0, 0:level_x] = values[:, 0, :]
        ysend[r, 1, 0:level_x] = values[:, cy - 1, :]
        pick = one_hot(iota((8, cz), 1) == jnp.where(iota((8, cz), 0) == 0, 0, cz - 1))
        pick = jnp.where(iota((8, cz), 0) < 2, pick, 0.0)
        zsend[r, :, 0:rows] = dot(pick, values.reshape(rows, cz), (((1,), (1,)), ((), ())))
        for exists, out, _ in copies(r, level_x):
            pl.when(exists)(out.start)

    def neighbours(r, values, step):
        level_x = values.shape[0]
        rows = level_x * cy
        row, lane = iota(values.shape, 1), iota(values.shape, 2)
        total = jnp.where(lane < step, 0.0, pltpu.roll(values, step, 2))
        total = total + jnp.where(lane >= cz - step, 0.0, pltpu.roll(values, cz - step, 2))
        up, down = pltpu.roll(values, step, 1), pltpu.roll(values, cy - step, 1)
        for exists, _, back in copies(r, level_x):
            pl.when(exists)(back.wait_recv)
        total = total + sum_x(values, xrecv[r, 0], xrecv[r, 1])
        low, high = yrecv[r, 0, 0:level_x], yrecv[r, 1, 0:level_x]
        total = total + jnp.where(row < step, low[:, None, :], up)
        total = total + jnp.where(row >= cy - step, high[:, None, :], down)
        halo = jnp.concatenate([zrecv[r, 0, :, 0:rows], zrecv[r, 1, :, 0:rows]], 0)
        slot, at = iota((16, cz), 0), iota((16, cz), 1)
        spread = one_hot(((slot == 1) & (at < step)) | ((slot == 8) & (at >= cz - step)))
        edge = dot(halo.T, spread)
        return total + edge.reshape(level_x, cy, cz)

    def sweep(values, around, source, scaled, coupling):
        return values * (1.0 - WEIGHT) + scaled * (source + coupling * around)

    diag0 = 6.0 + d0
    scaled0 = WEIGHT / diag0
    v = scaled0 * b0
    exchange(0, v)
    d1 = coarsen_dup(d0, 1)
    d2 = coarsen_dup(d1, 2)
    s0 = sweep(v, neighbours(0, v, 1), b0, scaled0, 1.0)
    exchange(1, s0)
    b1 = coarsen_dup(b0 - diag0 * s0 + neighbours(1, s0, 1), 1)

    diag1 = 1.5 + d1
    scaled1 = WEIGHT / diag1
    v = scaled1 * b1
    exchange(2, v)
    s1 = sweep(v, neighbours(2, v, 2), b1, scaled1, 0.25)
    exchange(3, s1)
    around1 = neighbours(3, s1, 2)
    b2 = coarsen_dup(b1 - diag1 * s1 + 0.25 * around1, 2)

    qx, qy, qz = cx // 4, cy // 4, cz // 4
    row, lane = iota((cz, cz), 0), iota((cz, cz), 1)
    for which, block in enumerate((b2, d2)):
        flat = jnp.zeros((cy, cz), jnp.float32)
        for x in range(qx):
            place_z = one_hot((lane // qz == x) & (row == 4 * (lane % qz)))
            flat = flat + dot(block[x], place_z)
        pick_y = one_hot(iota((8, cy), 1) == 4 * (iota((8, cy), 0) - which * qy))
        if which:
            pay[...] = packed + dot(pick_y * one_hot(iota((8, cy), 0) >= qy), flat)
        else:
            packed = dot(pick_y * one_hot(iota((8, cy), 0) < qy), flat)
    gathered[me] = pay[...]

    def gather_copy(k):
        return pltpu.make_async_remote_copy(
            pay, gathered.at[me], gssem.at[k], grsem.at[me], coords((me + k) % devices), MESH
        )

    @pl.loop(1, devices)
    def _(k):
        gather_copy(k).start()

    @pl.loop(1, devices)
    def _(k):
        origin = (me + devices - k) % devices
        pltpu.make_async_remote_copy(
            pay, gathered.at[origin], gssem.at[k], grsem.at[origin],
            coords((me + k) % devices), MESH,
        ).wait_recv()

    wide = gb.shape[2]
    valid = nz * qz
    per_tile = cz // qz
    blocks = gathered[...].reshape(nx, ny, nz, 8, cz)
    lane = iota((nx, ny, 8, cz), 3)
    for tile in range(wide // cz):
        for x in range(qx):
            total = jnp.zeros((nx, ny, 8, cz), jnp.float32)
            for spot in range(min(per_tile, nz - tile * per_tile)):
                shift = (qz * (spot - x)) % cz
                piece = blocks[:, :, tile * per_tile + spot]
                if shift:
                    piece = pltpu.roll(piece.reshape(nx * ny * 8, cz), shift, 1).reshape(
                        nx, ny, 8, cz
                    )
                total = jnp.where(lane // qz == spot, piece, total)
            for i in range(nx):
                for j in range(ny):
                    where = (qx * i + x, slice(qy * j, qy * j + qy), slice(tile * cz, tile * cz + cz))
                    gb[where] = total[i, j, 0:qy]
                    gd[where] = total[i, j, qy : 2 * qy]
    b2 = gb[...]
    d2 = gd[...]
    damping_mean = jnp.sum(jnp.sum(d2, 0, keepdims=True), axis=(1, 2), keepdims=True)[0] * (
        1.0 / (b2.shape[0] * b2.shape[1] * valid)
    )
    c2, c3 = 0.25**2, 0.25**3
    diag2 = 6.0 * c2 + d2
    scaled2 = WEIGHT / diag2
    v = scaled2 * b2
    s2 = sweep(v, neighbours_global(v, 1, valid), b2, scaled2, c2)
    near2 = neighbours_global(s2, 1, valid)
    b3 = coarsen_dup(b2 - diag2 * s2 + c2 * near2, 1)
    diag3 = 6.0 * c3 + coarsen_dup(d2, 1)
    scaled3 = WEIGHT / diag3
    v = scaled3 * b3
    s3 = sweep(v, neighbours_global(v, 2, valid), b3, scaled3, c3)
    near3 = neighbours_global(s3, 2, valid)
    rem = b3 - diag3 * s3 + c3 * near3

    bx = cx // 8
    rows = rem.shape[1]
    ty, tz = ty_ref[...], tz_ref[...]
    rem = rem.reshape(nx, bx, rows, wide)
    means = rem[:, 0]
    for i in range(1, bx):
        means = means + rem[:, i]
    means = dot(means.reshape(nx * rows, wide), tz).reshape(nx, rows, wide)
    means = [dot(ty, means[i]) for i in range(nx)]
    spectrum = []
    for a in range(nx):
        term = means[0] * float(table_x[a, 0] / bx)
        for i in range(1, nx):
            term = term + means[i] * float(table_x[a, i] / bx)
        spectrum.append(dot(ty, term / (den_ref[a] + damping_mean)))
    solved = []
    for i in range(nx):
        term = spectrum[0] * float(table_x[i, 0])
        for a in range(1, nx):
            term = term + spectrum[a] * float(table_x[i, a])
        solved.append(term)
    solved = dot(jnp.stack(solved).reshape(nx * rows, wide), tz).reshape(nx, rows, wide)

    v = s3 + expand_x(solved, bx)
    for _ in range(2):
        v = sweep(v, neighbours_global(v, 2, valid), b3, scaled3, c3)
    v = s2 + expand_x(v, 2)
    for _ in range(2):
        v = sweep(v, neighbours_global(v, 1, valid), b2, scaled2, c2)

    zero = jnp.zeros((1, rows, wide), jnp.float32)
    v2[0:1] = zero
    v2[pl.ds(1, qx * nx)] = v
    v2[pl.ds(1 + qx * nx, 1)] = zero
    part = v2[pl.ds(qx * gx, qx + 2)]
    k, at = iota((wide, cz), 0), iota((wide, cz), 1)
    inside = k < valid
    fine = at // 2 + gz * (cz // 2)
    own_z = one_hot(inside & (k == fine // 2))
    next_z = one_hot(inside & (k == (fine + 1) // 2)) + one_hot(
        inside & (k == (fine + 1) // 2 - 1)
    )
    at, k = iota((cy, rows), 0), iota((cy, rows), 1)
    fine = at // 2 + gy * (cy // 2)
    own_y = one_hot(k == fine // 2)
    next_y = one_hot(k == (fine + 1) // 2) + one_hot(k == (fine + 1) // 2 - 1)
    in_z = dot(part.reshape((qx + 2) * rows, wide), own_z).reshape(qx + 2, rows, cz)
    by_z = dot(part[1 : qx + 1].reshape(qx * rows, wide), next_z).reshape(qx, rows, cz)
    own = [dot(own_y, in_z[i]) for i in range(qx + 2)]
    side = [dot(next_y, in_z[i + 1]) + dot(own_y, by_z[i]) for i in range(qx)]
    correction = expand_x(jnp.stack(own[1:-1]), 2)
    near = expand_x(jnp.stack(side), 2) + sum_x(correction, own[0], own[-1])
    v = sweep(s1 + correction, around1 + near, b1, scaled1, 0.25)
    exchange(4, v)
    v = sweep(v, neighbours(4, v, 2), b1, scaled1, 0.25)

    v = s0 + expand_x(v, 2)
    exchange(5, v)
    v = sweep(v, neighbours(5, v, 1), b0, scaled0, 1.0)
    exchange(6, v)
    out_ref[...] = sweep(v, neighbours(6, v, 1), b0, scaled0, 1.0)

    for r in range(ROUNDS):
        for exists, out, _ in copies(r, cx // 2 if r in (2, 3, 4) else cx):
            pl.when(exists)(out.wait_send)

    @pl.loop(1, devices)
    def _(k):
        gather_copy(k).wait_send()


def sine_table(points):
    index = np.arange(1, points + 1)
    return math.sqrt(2.0 / (points + 1)) * np.sin(
        math.pi * index[:, None] * index[None, :] / (points + 1)
    )


def eigen_values(points, spacing):
    index = np.arange(1, points + 1)
    return (2.0 - 2.0 * np.cos(math.pi * index / (points + 1))) / (spacing * spacing)


def solution(mesh):
    nx, ny, nz = (mesh.shape[a] for a in AXES)

    def local(divergence, damping):
        cx, cy, cz = divergence.shape
        rows, valid = ny * (cy // 4), nz * (cz // 4)
        wide = -(-valid // cz) * cz
        spread_y, spread_z = cy // 4, cz // 4
        table_y = np.repeat(np.repeat(sine_table(ny), spread_y, 0), spread_y, 1) / spread_y
        table_z = np.zeros((wide, wide))
        table_z[:valid, :valid] = (
            np.repeat(np.repeat(sine_table(nz), spread_z, 0), spread_z, 1) / spread_z
        )
        den = np.ones((nx, rows, wide))
        den[:, :, :valid] = (
            eigen_values(nx, cx)[:, None, None]
            + np.repeat(eigen_values(ny, cy), spread_y)[None, :, None]
            + np.repeat(eigen_values(nz, cz), spread_z)[None, None, :]
        )
        tables = [jnp.asarray(t, jnp.float32) for t in (table_y, table_z, den)]
        f32 = jnp.float32
        devices = nx * ny * nz
        return pl.pallas_call(
            functools.partial(kernel, (cx, cy, cz), sine_table(nx)),
            out_shape=jax.ShapeDtypeStruct(divergence.shape, f32),
            in_specs=[pl.BlockSpec(memory_space=pltpu.VMEM)] * 5,
            out_specs=pl.BlockSpec(memory_space=pltpu.VMEM),
            scratch_shapes=[
                pltpu.VMEM((ROUNDS, 2, cy, cz), f32),
                pltpu.VMEM((ROUNDS, 2, cx, cz), f32),
                pltpu.VMEM((ROUNDS, 8, cx * cy), f32),
                pltpu.VMEM((ROUNDS, 2, cy, cz), f32),
                pltpu.VMEM((ROUNDS, 2, cx, cz), f32),
                pltpu.VMEM((ROUNDS, 2, 8, cx * cy), f32),
                pltpu.VMEM((8, cz), f32),
                pltpu.VMEM((devices, 8, cz), f32),
                pltpu.VMEM((nx * (cx // 4), rows, wide), f32),
                pltpu.VMEM((nx * (cx // 4), rows, wide), f32),
                pltpu.VMEM((nx * (cx // 4) + 2, rows, wide), f32),
                pltpu.SemaphoreType.DMA((ROUNDS, 6)),
                pltpu.SemaphoreType.DMA((ROUNDS, 6)),
                pltpu.SemaphoreType.DMA((devices,)),
                pltpu.SemaphoreType.DMA((devices,)),
            ],
            compiler_params=pltpu.CompilerParams(
                collective_id=0, has_side_effects=True, vmem_limit_bytes=60 * 1024 * 1024
            ),
        )(divergence, damping, *tables)

    spec = P(*AXES)
    return jax.shard_map(local, mesh=mesh, in_specs=(spec, spec), out_specs=spec, check_vma=False)
```

time: 366 us -> 43.7 us (0.12)
  starting transfers between devices: 179 us -> 0 us
  waiting for transfers between devices: 85.3 us -> 0 us
  blocking collectives: 47.4 us -> 0 us
  Pallas kernels: 0 us -> 42 us
  local copies, waits for them, and re-layouts: 27.7 us -> 1.57 us
  other arithmetic: 19.6 us -> 0 us
    ppermute x72 -> x0, starting transfers between devices: 179 us -> none  [the longest x36 132 us: with_halo(): lax.ppermute(lax.slice_in_dim(block, block.shape[dim] - width, None, axis...]
    ppermute x72 -> x0, waiting for transfers between devices: 85.3 us -> none  [the longest x36 50.3 us: with_halo(): lax.ppermute(lax.slice_in_dim(block, 0, width, axis=dim), axis, backward)]
    unnamed x1 -> x0, blocking collectives: 47.4 us -> none
    pallas_call x0 -> x1, Pallas kernels: none -> 42 us  [local(): pl.pallas_call(functools.partial(kernel, (cx, cy, cz), sine_table(nx)), o...]
    reshape x12 -> x0, local copies, waits for them, and re-layouts: 22.1 us -> none  [the longest x4 20.8 us: coarsen(): values.reshape(size_x // block_x, block_x, size_y // block_y, block_y, si...]
    reduce_sum x9 -> x0, other arithmetic: 10.6 us -> none  [the longest x6 8.56 us: coarsen(): return shaped.mean(axis=(1, 3, 5))]
  transfers between devices with their start and end apart: 72 -> 0, of which waited for: 45 -> 0; matrix products, arithmetic and copies ran while one was open for 5% -> 0% of each run, Pallas kernels for 0% -> 0%
where the time goes in v1:
time: 43.7 us; the launch traced here: 43.6 us
  Pallas kernels  42 us (96%)
  local copies, waits for them, and re-layouts  1.57 us (4%)
    pallas_call x1, Pallas kernels, local(): pl.pallas_call(functools.partial(kernel, (cx, cy, cz), sine_table(nx)), o...  42 us
    unnamed x1, local copies, waits for them, and re-layouts  1.57 us

profile of v1, /device:TPU:0, one launch (start us, length us, event | category | flops | bytes accessed | tf_op | source)
XLA Modules:
  0.0 43.6 jit_solution(2545144347268127332)
XLA Ops:
  0.0 42.0 %shard_map.55 = f32[16,16,128]{2,1,0:T(8,128)} custom-call(f32[16,16,128]{2,1,0:T(8,128)} %b_ref.1, f32[16,16,128]{2,1,0:T(8,128)} %d_ref.1, f32[16,16]{1,0:T(8,128)} %constant.6.clone.ty_ref, f32[128,128]{1,0:T(8,128)} %constant.7.clone.tz_ref, f32[4,16,128]{2,1,0:T(8,128)} %constant.8.clone.den_ref), custom_call_target="tpu_custom_call" | custom-call | tf_op jit(solution)/shard_map/pallas_call | solution.py:361
  42.0 1.6 %copy.7 = f32[16,16,128]{2,1,0:T(8,128)} copy(f32[16,16,128]{2,1,0:T(8,128)} %shard_map.55) | data formatting | bytes 262144

commit v2 on v1

--- a/solution.py
+++ b/solution.py
@@ -77,8 +77,29 @@
     size = {"gx": nx, "gy": ny, "gz": nz}
     me = (gx * ny + gy) * nz + gz
 
+    def shifted(position, by, count):
+        moved = position + by
+        return jnp.where(moved >= count, moved - count, moved)
+
+    along = {a: [shifted(place[a], k, size[a]) for k in range(size[a])] for a in AXES}
+    offsets = [(i, j, k) for i in range(nx) for j in range(ny) for k in range(nz)][1:]
+    offsets.sort(key=lambda o: -sum(min(d, n - d) for d, n in zip(o, (nx, ny, nz))))
+
+    def peer(offset):
+        return tuple(along[a][d] for a, d in zip(AXES, offset))
+
     def coords(index):
         return (index // (ny * nz), (index // nz) % ny, index % nz)
+
+    def for_peers(act):
+        if devices <= 64:
+            for number, offset in enumerate(offsets):
+                act(number, peer(offset), peer(tuple(-d % n for d, n in zip(offset, (nx, ny, nz)))))
+        else:
+
+            @pl.loop(1, devices)
+            def _(k):
+                act(k, coords((me + k) % devices), coords((me + devices - k) % devices))
 
     xrecv[...] = jnp.zeros_like(xrecv)
     yrecv[...] = jnp.zeros_like(yrecv)
@@ -86,79 +107,82 @@
 
     barrier = pltpu.get_barrier_semaphore()
 
-    @pl.loop(1, devices)
-    def _(k):
-        pl.semaphore_signal(
-            barrier, inc=1, device_id=coords((me + k) % devices), device_id_type=MESH
-        )
+    for_peers(lambda _, to, back: pl.semaphore_signal(barrier, 1, device_id=to, device_id_type=MESH))
 
     b0 = b_ref[...]
     d0 = d_ref[...]
-
-    pl.semaphore_wait(barrier, devices - 1)
 
     def copies(r, level_x):
         result = []
         for axis_number, (axis, send, recv, length) in enumerate(
-            (("gx", xsend, xrecv, cy), ("gy", ysend, yrecv, level_x), ("gz", zsend, zrecv, None))
+            (("gx", xsend, xrecv, cy), ("gy", ysend, yrecv, level_x), ("gz", zsend, zrecv, cy))
         ):
             for side in (0, 1):
                 other = 1 - side
                 index = 2 * axis_number
-                if length is None:
-                    src = send.at[r]
-                    there, here = recv.at[r, other], recv.at[r, side]
-                    if level_x * cy < send.shape[2]:
-                        cut = (slice(None), pl.ds(0, level_x * cy))
-                        src, there, here = src.at[cut], there.at[cut], here.at[cut]
-                else:
-                    cut = pl.ds(0, length)
-                    src = send.at[r, side, cut]
-                    there, here = recv.at[r, other, cut], recv.at[r, side, cut]
+                cut = pl.ds(0, length)
+                src = send.at[r, cut] if axis == "gz" else send.at[r, side, cut]
                 target = dict(place)
                 target[axis] = place[axis] + (1 if side else -1)
                 device = tuple(target[a] for a in AXES)
                 exists = place[axis] < size[axis] - 1 if side else place[axis] > 0
-                out = pltpu.make_async_remote_copy(
-                    src, there, ssem.at[r, index + side], rsem.at[r, index + other], device, MESH
+                sent = ssem.at[r, index + side]
+                out = functools.partial(
+                    pltpu.make_async_remote_copy,
+                    src, recv.at[r, other, cut], sent, rsem.at[r, index + other], device, MESH,
                 )
-                back = pltpu.make_async_remote_copy(
-                    src, here, ssem.at[r, index + side], rsem.at[r, index + side], device, MESH
+                back = functools.partial(
+                    pltpu.make_async_remote_copy,
+                    src, recv.at[r, side, cut], sent, rsem.at[r, index + side], device, MESH,
                 )
                 result.append((exists, out, back))
         return result
 
-    def exchange(r, values):
+    def pack(r, values, step):
         level_x = values.shape[0]
-        rows = level_x * cy
         xsend[r, 0] = values[0]
         xsend[r, 1] = values[-1]
         ysend[r, 0, 0:level_x] = values[:, 0, :]
         ysend[r, 1, 0:level_x] = values[:, cy - 1, :]
-        pick = one_hot(iota((8, cz), 1) == jnp.where(iota((8, cz), 0) == 0, 0, cz - 1))
-        pick = jnp.where(iota((8, cz), 0) < 2, pick, 0.0)
-        zsend[r, :, 0:rows] = dot(pick, values.reshape(rows, cz), (((1,), (1,)), ((), ())))
+        lane = iota((cy, cz), 1)
+        both = jnp.zeros((cy, cz), jnp.float32)
+        for x in range(level_x):
+            both = jnp.where(
+                lane // (2 * step) == x, pltpu.roll(values[x], 2 * step * x + step, 1), both
+            )
+        zsend[r] = both
+
+    def send(r, level_x):
         for exists, out, _ in copies(r, level_x):
-            pl.when(exists)(out.start)
+            pl.when(exists)(lambda: out().start())
+
+    def exchange(r, values, step):
+        pack(r, values, step)
+        send(r, values.shape[0])
 
     def neighbours(r, values, step):
         level_x = values.shape[0]
-        rows = level_x * cy
         row, lane = iota(values.shape, 1), iota(values.shape, 2)
-        total = jnp.where(lane < step, 0.0, pltpu.roll(values, step, 2))
-        total = total + jnp.where(lane >= cz - step, 0.0, pltpu.roll(values, cz - step, 2))
+        before, after = pltpu.roll(values, step, 2), pltpu.roll(values, cz - step, 2)
         up, down = pltpu.roll(values, step, 1), pltpu.roll(values, cy - step, 1)
         for exists, _, back in copies(r, level_x):
-            pl.when(exists)(back.wait_recv)
+            pl.when(exists)(lambda: back().wait_recv())
+        flat_lane = iota((cy, cz), 1)
+        both = jnp.where(
+            (flat_lane // step) % 2 == 0,
+            pltpu.roll(zrecv[r, 1], cz - step, 1),
+            pltpu.roll(zrecv[r, 0], step, 1),
+        )
+        edge = jnp.stack(
+            [pltpu.roll(both, cz - 2 * step * x - step, 1) for x in range(level_x)]
+        )
+        total = jnp.where(lane < step, edge, before)
+        total = total + jnp.where(lane >= cz - step, edge, after)
         total = total + sum_x(values, xrecv[r, 0], xrecv[r, 1])
         low, high = yrecv[r, 0, 0:level_x], yrecv[r, 1, 0:level_x]
         total = total + jnp.where(row < step, low[:, None, :], up)
         total = total + jnp.where(row >= cy - step, high[:, None, :], down)
-        halo = jnp.concatenate([zrecv[r, 0, :, 0:rows], zrecv[r, 1, :, 0:rows]], 0)
-        slot, at = iota((16, cz), 0), iota((16, cz), 1)
-        spread = one_hot(((slot == 1) & (at < step)) | ((slot == 8) & (at >= cz - step)))
-        edge = dot(halo.T, spread)
-        return total + edge.reshape(level_x, cy, cz)
+        return total
 
     def sweep(values, around, source, scaled, coupling):
         return values * (1.0 - WEIGHT) + scaled * (source + coupling * around)
@@ -166,19 +190,21 @@
     diag0 = 6.0 + d0
     scaled0 = WEIGHT / diag0
     v = scaled0 * b0
-    exchange(0, v)
+    pack(0, v, 1)
     d1 = coarsen_dup(d0, 1)
     d2 = coarsen_dup(d1, 2)
+    pl.semaphore_wait(barrier, devices - 1)
+    send(0, cx)
     s0 = sweep(v, neighbours(0, v, 1), b0, scaled0, 1.0)
-    exchange(1, s0)
+    exchange(1, s0, 1)
     b1 = coarsen_dup(b0 - diag0 * s0 + neighbours(1, s0, 1), 1)
 
     diag1 = 1.5 + d1
     scaled1 = WEIGHT / diag1
     v = scaled1 * b1
-    exchange(2, v)
+    exchange(2, v, 2)
     s1 = sweep(v, neighbours(2, v, 2), b1, scaled1, 0.25)
-    exchange(3, s1)
+    exchange(3, s1, 2)
     around1 = neighbours(3, s1, 2)
     b2 = coarsen_dup(b1 - diag1 * s1 + 0.25 * around1, 2)
 
@@ -196,22 +222,19 @@
             packed = dot(pick_y * one_hot(iota((8, cy), 0) < qy), flat)
     gathered[me] = pay[...]
 
-    def gather_copy(k):
+    def gather_copy(number, to):
         return pltpu.make_async_remote_copy(
-            pay, gathered.at[me], gssem.at[k], grsem.at[me], coords((me + k) % devices), MESH
-        )
-
-    @pl.loop(1, devices)
-    def _(k):
-        gather_copy(k).start()
-
-    @pl.loop(1, devices)
-    def _(k):
-        origin = (me + devices - k) % devices
+            pay, gathered.at[me], gssem.at[number], grsem.at[me], to, MESH
+        )
+
+    def gather_wait(number, to, back):
+        origin = (back[0] * ny + back[1]) * nz + back[2]
         pltpu.make_async_remote_copy(
-            pay, gathered.at[origin], gssem.at[k], grsem.at[origin],
-            coords((me + k) % devices), MESH,
+            pay, gathered.at[origin], gssem.at[number], grsem.at[origin], to, MESH
         ).wait_recv()
+
+    for_peers(lambda number, to, back: gather_copy(number, to).start())
+    for_peers(gather_wait)
 
     wide = gb.shape[2]
     valid = nz * qz
@@ -306,22 +329,20 @@
     correction = expand_x(jnp.stack(own[1:-1]), 2)
     near = expand_x(jnp.stack(side), 2) + sum_x(correction, own[0], own[-1])
     v = sweep(s1 + correction, around1 + near, b1, scaled1, 0.25)
-    exchange(4, v)
+    exchange(4, v, 2)
     v = sweep(v, neighbours(4, v, 2), b1, scaled1, 0.25)
 
     v = s0 + expand_x(v, 2)
-    exchange(5, v)
+    exchange(5, v, 1)
     v = sweep(v, neighbours(5, v, 1), b0, scaled0, 1.0)
-    exchange(6, v)
+    exchange(6, v, 1)
     out_ref[...] = sweep(v, neighbours(6, v, 1), b0, scaled0, 1.0)
 
     for r in range(ROUNDS):
         for exists, out, _ in copies(r, cx // 2 if r in (2, 3, 4) else cx):
-            pl.when(exists)(out.wait_send)
-
-    @pl.loop(1, devices)
-    def _(k):
-        gather_copy(k).wait_send()
+            pl.when(exists)(lambda: out().wait_send())
+
+    for_peers(lambda number, to, back: gather_copy(number, to).wait_send())
 
 
 def sine_table(points):
@@ -366,10 +387,10 @@
             scratch_shapes=[
                 pltpu.VMEM((ROUNDS, 2, cy, cz), f32),
                 pltpu.VMEM((ROUNDS, 2, cx, cz), f32),
-                pltpu.VMEM((ROUNDS, 8, cx * cy), f32),
+                pltpu.VMEM((ROUNDS, cy, cz), f32),
                 pltpu.VMEM((ROUNDS, 2, cy, cz), f32),
                 pltpu.VMEM((ROUNDS, 2, cx, cz), f32),
-                pltpu.VMEM((ROUNDS, 2, 8, cx * cy), f32),
+                pltpu.VMEM((ROUNDS, 2, cy, cz), f32),
                 pltpu.VMEM((8, cz), f32),
                 pltpu.VMEM((devices, 8, cz), f32),
                 pltpu.VMEM((nx * (cx // 4), rows, wide), f32),

time: 43.7 us -> 40.1 us (0.918)
  Pallas kernels: 42 us -> 38.4 us
    pallas_call x1, Pallas kernels: 42 us -> 38.4 us  [local(): pl.pallas_call(functools.partial(kernel, (cx, cy, cz), sine_table(nx)), o...]
where the time goes in v2:
time: 40.1 us; the launch traced here: 40 us
  Pallas kernels  38.4 us (96%)
  local copies, waits for them, and re-layouts  1.57 us (4%)
    pallas_call x1, Pallas kernels, local(): pl.pallas_call(functools.partial(kernel, (cx, cy, cz), sine_table(nx)), o...  38.4 us
    unnamed x1, local copies, waits for them, and re-layouts  1.57 us

profile of v2, /device:TPU:0, one launch (start us, length us, event | category | flops | bytes accessed | tf_op | source)
XLA Modules:
  0.0 40.0 jit_solution(7342813596868845694)
XLA Ops:
  0.0 38.4 %shard_map.55 = f32[16,16,128]{2,1,0:T(8,128)} custom-call(f32[16,16,128]{2,1,0:T(8,128)} %b_ref.1, f32[16,16,128]{2,1,0:T(8,128)} %d_ref.1, f32[16,16]{1,0:T(8,128)} %constant.6.clone.ty_ref, f32[128,128]{1,0:T(8,128)} %constant.7.clone.tz_ref, f32[4,16,128]{2,1,0:T(8,128)} %constant.8.clone.den_ref), custom_call_target="tpu_custom_call" | custom-call | tf_op jit(solution)/shard_map/pallas_call | solution.py:382
  38.4 1.6 %copy.7 = f32[16,16,128]{2,1,0:T(8,128)} copy(f32[16,16,128]{2,1,0:T(8,128)} %shard_map.55) | data formatting | bytes 262144

commit v3 on v2

--- a/solution.py
+++ b/solution.py
@@ -10,7 +10,7 @@
 from jax.sharding import PartitionSpec as P
 
 AXES = ("gx", "gy", "gz")
-ROUNDS = 7
+ROUNDS = 8
 WEIGHT = 2.0 / 3.0
 MESH = pl.DeviceIdType.MESH
 HIGH = lax.Precision.HIGHEST
@@ -160,11 +160,7 @@
         pack(r, values, step)
         send(r, values.shape[0])
 
-    def neighbours(r, values, step):
-        level_x = values.shape[0]
-        row, lane = iota(values.shape, 1), iota(values.shape, 2)
-        before, after = pltpu.roll(values, step, 2), pltpu.roll(values, cz - step, 2)
-        up, down = pltpu.roll(values, step, 1), pltpu.roll(values, cy - step, 1)
+    def receive(r, level_x, step):
         for exists, _, back in copies(r, level_x):
             pl.when(exists)(lambda: back().wait_recv())
         flat_lane = iota((cy, cz), 1)
@@ -176,13 +172,30 @@
         edge = jnp.stack(
             [pltpu.roll(both, cz - 2 * step * x - step, 1) for x in range(level_x)]
         )
+        return (
+            xrecv[r, 0], xrecv[r, 1], yrecv[r, 0, 0:level_x], yrecv[r, 1, 0:level_x], edge,
+        )
+
+    def inner(values, step):
+        return (
+            pltpu.roll(values, step, 2), pltpu.roll(values, cz - step, 2),
+            pltpu.roll(values, step, 1), pltpu.roll(values, cy - step, 1),
+        )
+
+    def add_up(values, rolled, faces, step):
+        row, lane = iota(values.shape, 1), iota(values.shape, 2)
+        before, after, up, down = rolled
+        x_low, x_high, low, high, edge = faces
         total = jnp.where(lane < step, edge, before)
         total = total + jnp.where(lane >= cz - step, edge, after)
-        total = total + sum_x(values, xrecv[r, 0], xrecv[r, 1])
-        low, high = yrecv[r, 0, 0:level_x], yrecv[r, 1, 0:level_x]
+        total = total + sum_x(values, x_low, x_high)
         total = total + jnp.where(row < step, low[:, None, :], up)
         total = total + jnp.where(row >= cy - step, high[:, None, :], down)
         return total
+
+    def neighbours(r, values, step):
+        rolled = inner(values, step)
+        return add_up(values, rolled, receive(r, values.shape[0], step), step)
 
     def sweep(values, around, source, scaled, coupling):
         return values * (1.0 - WEIGHT) + scaled * (source + coupling * around)
@@ -195,12 +208,13 @@
     d2 = coarsen_dup(d1, 2)
     pl.semaphore_wait(barrier, devices - 1)
     send(0, cx)
+    diag1 = 1.5 + d1
+    scaled1 = WEIGHT / diag1
+    exchange(4, scaled1, 2)
     s0 = sweep(v, neighbours(0, v, 1), b0, scaled0, 1.0)
     exchange(1, s0, 1)
     b1 = coarsen_dup(b0 - diag0 * s0 + neighbours(1, s0, 1), 1)
 
-    diag1 = 1.5 + d1
-    scaled1 = WEIGHT / diag1
     v = scaled1 * b1
     exchange(2, v, 2)
     s1 = sweep(v, neighbours(2, v, 2), b1, scaled1, 0.25)
@@ -234,6 +248,9 @@
         ).wait_recv()
 
     for_peers(lambda number, to, back: gather_copy(number, to).start())
+
+    swept1 = sweep(s1, around1, b1, scaled1, 0.25)
+    exchange(7, swept1, 2)
     for_peers(gather_wait)
 
     wide = gb.shape[2]
@@ -311,26 +328,43 @@
     v2[pl.ds(1, qx * nx)] = v
     v2[pl.ds(1 + qx * nx, 1)] = zero
     part = v2[pl.ds(qx * gx, qx + 2)]
-    k, at = iota((wide, cz), 0), iota((wide, cz), 1)
-    inside = k < valid
-    fine = at // 2 + gz * (cz // 2)
-    own_z = one_hot(inside & (k == fine // 2))
-    next_z = one_hot(inside & (k == (fine + 1) // 2)) + one_hot(
-        inside & (k == (fine + 1) // 2 - 1)
+    k, at = iota((wide, 2 * cz), 0), iota((wide, 2 * cz), 1)
+    inside, first = k < valid, gz * (cz // 2)
+    beside = jnp.where(at < cz + 2, first - 1, first + cz // 2)
+    fine = jnp.where(at < cz, at // 2 + first, beside)
+    inside = inside & ((at < cz + 2) | (at >= 2 * cz - 2))
+    own_z = one_hot(inside & (k == (fine >> 1)))
+    next_z = one_hot(inside & (k == (fine + 1) >> 1)) + one_hot(
+        inside & (k == ((fine + 1) >> 1) - 1)
     )
-    at, k = iota((cy, rows), 0), iota((cy, rows), 1)
-    fine = at // 2 + gy * (cy // 2)
-    own_y = one_hot(k == fine // 2)
-    next_y = one_hot(k == (fine + 1) // 2) + one_hot(k == (fine + 1) // 2 - 1)
-    in_z = dot(part.reshape((qx + 2) * rows, wide), own_z).reshape(qx + 2, rows, cz)
-    by_z = dot(part[1 : qx + 1].reshape(qx * rows, wide), next_z).reshape(qx, rows, cz)
-    own = [dot(own_y, in_z[i]) for i in range(qx + 2)]
-    side = [dot(next_y, in_z[i + 1]) + dot(own_y, by_z[i]) for i in range(qx)]
-    correction = expand_x(jnp.stack(own[1:-1]), 2)
-    near = expand_x(jnp.stack(side), 2) + sum_x(correction, own[0], own[-1])
-    v = sweep(s1 + correction, around1 + near, b1, scaled1, 0.25)
-    exchange(4, v, 2)
-    v = sweep(v, neighbours(4, v, 2), b1, scaled1, 0.25)
+    at, k = iota((cy + 8, rows), 0), iota((cy + 8, rows), 1)
+    first = gy * (cy // 2)
+    fine = jnp.where(at < cy, at // 2 + first, jnp.where(at == cy, first - 1, first + cy // 2))
+    own_y = one_hot(k == (fine >> 1))
+    next_y = one_hot(k == (fine + 1) >> 1) + one_hot(k == ((fine + 1) >> 1) - 1)
+    flat = part.reshape((qx + 2) * rows, wide)
+    in_z = dot(flat, own_z).reshape(qx + 2, rows, 2 * cz)
+    by_z = dot(flat, next_z).reshape(qx + 2, rows, 2 * cz)
+    own = jnp.stack([dot(own_y, in_z[i]) for i in range(qx + 2)])
+    side = jnp.stack([dot(next_y, in_z[i]) + dot(own_y, by_z[i]) for i in range(qx + 2)])
+    own, side = expand_x(own, 2), expand_x(side, 2)
+    near = side[1:-1] + own[:-2] + own[2:]
+    own = own[1:-1]
+    faces, scales = receive(7, cx // 2, 2), receive(4, cx // 2, 2)
+    spots = (
+        (0, slice(0, cy), slice(0, cz)),
+        (-1, slice(0, cy), slice(0, cz)),
+        (slice(1, -1), cy, slice(0, cz)),
+        (slice(1, -1), cy + 1, slice(0, cz)),
+        (slice(1, -1), slice(0, cy), slice(cz, 2 * cz)),
+    )
+
+    def swept(base, scaled, spot):
+        return base + own[spot] * (1.0 - WEIGHT) + scaled * (0.25 * near[spot])
+
+    v = swept(swept1, scaled1, (slice(1, -1), slice(0, cy), slice(0, cz)))
+    faces = [swept(f, g, spot) for f, g, spot in zip(faces, scales, spots)]
+    v = sweep(v, add_up(v, inner(v, 2), faces, 2), b1, scaled1, 0.25)
 
     v = s0 + expand_x(v, 2)
     exchange(5, v, 1)
@@ -339,7 +373,7 @@
     out_ref[...] = sweep(v, neighbours(6, v, 1), b0, scaled0, 1.0)
 
     for r in range(ROUNDS):
-        for exists, out, _ in copies(r, cx // 2 if r in (2, 3, 4) else cx):
+        for exists, out, _ in copies(r, cx // 2 if r in (2, 3, 4, 7) else cx):
             pl.when(exists)(lambda: out().wait_send())
 
     for_peers(lambda number, to, back: gather_copy(number, to).wait_send())

time: 40.1 us -> 37.9 us (0.945)
  Pallas kernels: 38.4 us -> 36.2 us
    pallas_call x1, Pallas kernels: 38.4 us -> 36.2 us  [local(): pl.pallas_call(functools.partial(kernel, (cx, cy, cz), sine_table(nx)), o...]
where the time goes in v3:
time: 37.9 us; the launch traced here: 37.8 us
  Pallas kernels  36.2 us (96%)
  local copies, waits for them, and re-layouts  1.57 us (4%)
    pallas_call x1, Pallas kernels, local(): pl.pallas_call(functools.partial(kernel, (cx, cy, cz), sine_table(nx)), o...  36.2 us
    unnamed x1, local copies, waits for them, and re-layouts  1.57 us

profile of v3, /device:TPU:0, one launch (start us, length us, event | category | flops | bytes accessed | tf_op | source)
XLA Modules:
  0.0 37.8 jit_solution(15797527516708588395)
XLA Ops:
  0.0 36.2 %shard_map.55 = f32[16,16,128]{2,1,0:T(8,128)} custom-call(f32[16,16,128]{2,1,0:T(8,128)} %b_ref.1, f32[16,16,128]{2,1,0:T(8,128)} %d_ref.1, f32[16,16]{1,0:T(8,128)} %constant.6.clone.ty_ref, f32[128,128]{1,0:T(8,128)} %constant.7.clone.tz_ref, f32[4,16,128]{2,1,0:T(8,128)} %constant.8.clone.den_ref), custom_call_target="tpu_custom_call" | custom-call | tf_op jit(solution)/shard_map/pallas_call | solution.py:416
  36.2 1.6 %copy.7 = f32[16,16,128]{2,1,0:T(8,128)} copy(f32[16,16,128]{2,1,0:T(8,128)} %shard_map.55) | data formatting | bytes 262144

commit v4 on v3

--- a/solution.py
+++ b/solution.py
@@ -65,7 +65,7 @@
 
 def kernel(
     counts, tables, b_ref, d_ref, ty_ref, tz_ref, den_ref, out_ref,
-    xsend, ysend, zsend, xrecv, yrecv, zrecv, pay, gathered, gb, gd, v2,
+    xsend, ysend, zsend, xrecv, yrecv, zrecv, pay, gathered, joined, gb, gd, v2,
     ssem, rsem, gssem, grsem,
 ):
     cx, cy, cz = counts
@@ -200,17 +200,49 @@
     def sweep(values, around, source, scaled, coupling):
         return values * (1.0 - WEIGHT) + scaled * (source + coupling * around)
 
+    qx, qy, qz = cx // 4, cy // 4, cz // 4
+
+    def flatten(which, block):
+        row, lane = iota((cz, cz), 0), iota((cz, cz), 1)
+        flat = jnp.zeros((cy, cz), jnp.float32)
+        for x in range(qx):
+            place_z = one_hot((lane // qz == x) & (row == 4 * (lane % qz)))
+            flat = flat + dot(block[x], place_z)
+        pick_y = one_hot(iota((8, cy), 1) == 4 * iota((8, cy), 0))
+        pay[which] = dot(pick_y, flat)[0:qy]
+        gathered[which, me] = pay[which]
+
+    def gather_copy(which, number, to):
+        return pltpu.make_async_remote_copy(
+            pay.at[which], gathered.at[which, me],
+            gssem.at[number], grsem.at[which, me], to, MESH,
+        )
+
+    def gather_wait(which, number, to, back):
+        origin = (back[0] * ny + back[1]) * nz + back[2]
+        pltpu.make_async_remote_copy(
+            pay.at[which], gathered.at[which, origin],
+            gssem.at[number], grsem.at[which, origin], to, MESH,
+        ).wait_recv()
+
+    def sent(r):
+        for exists, out, _ in copies(r, cx // 2 if r in (2, 3, 4, 7) else cx):
+            pl.when(exists)(lambda: out().wait_send())
+
     diag0 = 6.0 + d0
     scaled0 = WEIGHT / diag0
     v = scaled0 * b0
     pack(0, v, 1)
     d1 = coarsen_dup(d0, 1)
     d2 = coarsen_dup(d1, 2)
+    diag1 = 1.5 + d1
+    scaled1 = WEIGHT / diag1
+    pack(4, scaled1, 2)
+    flatten(1, d2)
     pl.semaphore_wait(barrier, devices - 1)
     send(0, cx)
-    diag1 = 1.5 + d1
-    scaled1 = WEIGHT / diag1
-    exchange(4, scaled1, 2)
+    send(4, cx // 2)
+    for_peers(lambda number, to, back: gather_copy(1, number, to).start())
     s0 = sweep(v, neighbours(0, v, 1), b0, scaled0, 1.0)
     exchange(1, s0, 1)
     b1 = coarsen_dup(b0 - diag0 * s0 + neighbours(1, s0, 1), 1)
@@ -219,44 +251,27 @@
     exchange(2, v, 2)
     s1 = sweep(v, neighbours(2, v, 2), b1, scaled1, 0.25)
     exchange(3, s1, 2)
+    for_peers(lambda number, to, back: gather_copy(1, number, to).wait_send())
     around1 = neighbours(3, s1, 2)
     b2 = coarsen_dup(b1 - diag1 * s1 + 0.25 * around1, 2)
 
-    qx, qy, qz = cx // 4, cy // 4, cz // 4
-    row, lane = iota((cz, cz), 0), iota((cz, cz), 1)
-    for which, block in enumerate((b2, d2)):
-        flat = jnp.zeros((cy, cz), jnp.float32)
-        for x in range(qx):
-            place_z = one_hot((lane // qz == x) & (row == 4 * (lane % qz)))
-            flat = flat + dot(block[x], place_z)
-        pick_y = one_hot(iota((8, cy), 1) == 4 * (iota((8, cy), 0) - which * qy))
-        if which:
-            pay[...] = packed + dot(pick_y * one_hot(iota((8, cy), 0) >= qy), flat)
-        else:
-            packed = dot(pick_y * one_hot(iota((8, cy), 0) < qy), flat)
-    gathered[me] = pay[...]
-
-    def gather_copy(number, to):
-        return pltpu.make_async_remote_copy(
-            pay, gathered.at[me], gssem.at[number], grsem.at[me], to, MESH
-        )
-
-    def gather_wait(number, to, back):
-        origin = (back[0] * ny + back[1]) * nz + back[2]
-        pltpu.make_async_remote_copy(
-            pay, gathered.at[origin], gssem.at[number], grsem.at[origin], to, MESH
-        ).wait_recv()
-
-    for_peers(lambda number, to, back: gather_copy(number, to).start())
+    flatten(0, b2)
+    for_peers(lambda number, to, back: gather_copy(0, number, to).start())
+    for r in range(5):
+        sent(r)
 
     swept1 = sweep(s1, around1, b1, scaled1, 0.25)
     exchange(7, swept1, 2)
-    for_peers(gather_wait)
+    for_peers(functools.partial(gather_wait, 1))
+    for_peers(functools.partial(gather_wait, 0))
+    for index in range(devices):
+        joined[index, 0:qy] = gathered[0, index]
+        joined[index, qy : 2 * qy] = gathered[1, index]
 
     wide = gb.shape[2]
     valid = nz * qz
     per_tile = cz // qz
-    blocks = gathered[...].reshape(nx, ny, nz, 8, cz)
+    blocks = joined[...].reshape(nx, ny, nz, 8, cz)
     lane = iota((nx, ny, 8, cz), 3)
     for tile in range(wide // cz):
         for x in range(qx):
@@ -368,15 +383,14 @@
 
     v = s0 + expand_x(v, 2)
     exchange(5, v, 1)
+    for_peers(lambda number, to, back: gather_copy(0, number, to).wait_send())
+    sent(7)
     v = sweep(v, neighbours(5, v, 1), b0, scaled0, 1.0)
     exchange(6, v, 1)
+    sent(5)
     out_ref[...] = sweep(v, neighbours(6, v, 1), b0, scaled0, 1.0)
 
-    for r in range(ROUNDS):
-        for exists, out, _ in copies(r, cx // 2 if r in (2, 3, 4, 7) else cx):
-            pl.when(exists)(lambda: out().wait_send())
-
-    for_peers(lambda number, to, back: gather_copy(number, to).wait_send())
+    sent(6)
 
 
 def sine_table(points):
@@ -425,7 +439,8 @@
                 pltpu.VMEM((ROUNDS, 2, cy, cz), f32),
                 pltpu.VMEM((ROUNDS, 2, cx, cz), f32),
                 pltpu.VMEM((ROUNDS, 2, cy, cz), f32),
-                pltpu.VMEM((8, cz), f32),
+                pltpu.VMEM((2, cy // 4, cz), f32),
+                pltpu.VMEM((2, devices, cy // 4, cz), f32),
                 pltpu.VMEM((devices, 8, cz), f32),
                 pltpu.VMEM((nx * (cx // 4), rows, wide), f32),
                 pltpu.VMEM((nx * (cx // 4), rows, wide), f32),
@@ -433,7 +448,7 @@
                 pltpu.SemaphoreType.DMA((ROUNDS, 6)),
                 pltpu.SemaphoreType.DMA((ROUNDS, 6)),
                 pltpu.SemaphoreType.DMA((devices,)),
-                pltpu.SemaphoreType.DMA((devices,)),
+                pltpu.SemaphoreType.DMA((2, devices)),
             ],
             compiler_params=pltpu.CompilerParams(
                 collective_id=0, has_side_effects=True, vmem_limit_bytes=60 * 1024 * 1024

time: 37.9 us -> 37.8 us (level)
  no operation moved by 1% of the time
where the time goes in v4:
time: 37.8 us; the launch traced here: 37.6 us
  Pallas kernels  36 us (95%)
  local copies, waits for them, and re-layouts  1.57 us (4%)
    pallas_call x1, Pallas kernels, local(): pl.pallas_call(functools.partial(kernel, (cx, cy, cz), sine_table(nx)), o...  36 us
    unnamed x1, local copies, waits for them, and re-layouts  1.57 us

profile of v4, /device:TPU:0, one launch (start us, length us, event | category | flops | bytes accessed | tf_op | source)
XLA Modules:
  0.0 37.6 jit_solution(13413323929005312446)
XLA Ops:
  0.0 36.0 %shard_map.55 = f32[16,16,128]{2,1,0:T(8,128)} custom-call(f32[16,16,128]{2,1,0:T(8,128)} %b_ref.1, f32[16,16,128]{2,1,0:T(8,128)} %d_ref.1, f32[16,16]{1,0:T(8,128)} %constant.6.clone.ty_ref, f32[128,128]{1,0:T(8,128)} %constant.7.clone.tz_ref, f32[4,16,128]{2,1,0:T(8,128)} %constant.8.clone.den_ref), custom_call_target="tpu_custom_call" | custom-call | tf_op jit(solution)/shard_map/pallas_call | solution.py:430
  36.0 1.6 %copy.7 = f32[16,16,128]{2,1,0:T(8,128)} copy(f32[16,16,128]{2,1,0:T(8,128)} %shard_map.55) | data formatting | bytes 262144
